TPU v7x, 32 devices: a whole 2x2x4 slice. The times are simulated.
32 devices in a mesh: farcp: 4 (over x, core), nearcp: 4 (over z), heads: 2 (over y).
Axes of the slice: x: 2, y: 2, z: 4, core: 2. Of those that a mesh axis runs over, the one named last changes fastest.
Arguments:
- raw_keys: bfloat16 [16, 24576, 8, 128], P(None, ('farcp', 'nearcp'), 'heads'), may hold values from -6 to 6
- raw_values: bfloat16 [16, 24576, 8, 128], P(None, ('farcp', 'nearcp'), 'heads'), may hold values from -6 to 6
- turn_angle: float32 [24576, 64], replicated, may hold values from -3.140625 to 3.140625
Outputs:
- stored_keys: bfloat16 [16, 8, 128, 24576], P(('farcp', 'nearcp'), 'heads')
- stored_values: bfloat16 [16, 24576, 8, 128], P(('farcp', 'nearcp'), None, 'heads')
- page_high: bfloat16 [16, 384, 8, 128], P(('farcp', 'nearcp'), None, 'heads')
- page_low: bfloat16 [16, 384, 8, 128], P(('farcp', 'nearcp'), None, 'heads')
All inputs are finite; a program needn't handle non-finite values.
Results may differ from a plain program's by a relative error of at most 0.001.
Values may be sent and summed in bfloat16 or wider, within the bound.
A program may use at most 256 MiB of HBM per device.

v0:
```python
import jax
import jax.numpy as jnp
from jax import lax
from jax.sharding import PartitionSpec as P

PAGE = 64


def apply_rotary(vectors, angle):
    half = vectors.shape[-1] // 2
    cosine, sine = (jnp.cos(angle)[None, :, None, :], jnp.sin(angle)[None, :, None, :])
    first, second = (vectors[..., :half], vectors[..., half:])
    return jnp.concatenate(
        [first * cosine - second * sine, second * cosine + first * sine], axis=-1
    )


def keys_in_place(plain_keys, angle):
    wide_keys = plain_keys.astype(jnp.float32)
    return apply_rotary(wide_keys, angle)


def per_device(raw_keys, raw_values, turn_angle):
    my_angles = lax.dynamic_slice_in_dim(
        turn_angle, lax.axis_index(("farcp", "nearcp")) * raw_keys.shape[1], raw_keys.shape[1]
    )
    sent_keys = keys_in_place(raw_keys, my_angles).astype(jnp.bfloat16)
    moved_keys, stored_values = (
        lax.all_to_all(sent_keys, ("farcp", "nearcp"), split_axis=0, concat_axis=1, tiled=True),
        lax.all_to_all(raw_values, ("farcp", "nearcp"), split_axis=0, concat_axis=1, tiled=True),
    )
    page_view = moved_keys.reshape(
        moved_keys.shape[0], -1, PAGE, moved_keys.shape[2], moved_keys.shape[3]
    )
    page_high = jnp.max(page_view, axis=2)
    page_low = jnp.min(page_view, axis=2)
    stored_keys = jnp.transpose(moved_keys, (0, 2, 3, 1))
    return (stored_keys, stored_values, page_high, page_low)


def solution(mesh):
    return jax.shard_map(
        per_device,
        mesh=mesh,
        in_specs=(
            P(None, ("farcp", "nearcp"), "heads", None),
            P(None, ("farcp", "nearcp"), "heads", None),
            P(),
        ),
        out_specs=(
            P(("farcp", "nearcp"), "heads", None, None),
            P(("farcp", "nearcp"), None, "heads", None),
            P(("farcp", "nearcp"), None, "heads", None),
            P(("farcp", "nearcp"), None, "heads", None),
        ),
        check_vma=False,
    )
```

profile of v0, /device:TPU:4, one launch (start us, length us, event | category | flops | bytes accessed | tf_op | source)
XLA Modules:
  0.0 1232.2 jit_solution(8686672545005040533)
XLA Ops:
  0.6 2.3 dynamic-slice_cosine_fusion
  3.0 0.3 copy.7
  3.2 0.3 copy.8
  3.5 23.9 %convert_element_type.4 = f32[16,1536,4,128]{3,2,1,0:T(4,128)} convert(bf16[16,1536,4,128]{3,2,1,0:T(4,128)(2,1)} %param.3) | non-fusion elementwise | flops 12582912 | bytes 75497472 | tf_op jit(solution)/shard_map/convert_element_type | solution.py:19
  27.5 49.4 %subtract_convert_fusion = (bf16[16,1536,4,64]{3,2,1,0:T(4,128)(2,1)}, bf16[16,1536,4,64]{3,2,1,0:T(4,128)(2,1)}) fusion(f32[16,1536,4,128]{3,2,1,0:T(4,128)} %convert_element_type.4, f32[1536,64]{1,0:T(8,128)S(1)} %copy.8, f32[1536,64]{1,0:T(8,128)S(1)} %copy.7), kind=kLoop, calls=%fused_computation.1 | loop fusion | flops 50331648 | bytes 76283904 | tf_op jit(solution)/shard_map/convert
  76.9 37.5 %pad_maximum_fusion = bf16[16,1536,4,128]{3,2,1,0:T(4,128)(2,1)} fusion(bf16[16,1536,4,64]{3,2,1,0:T(4,128)(2,1)} %get-tuple-element.7, bf16[16,1536,4,64]{3,2,1,0:T(4,128)(2,1)} %get-tuple-element.6), kind=kLoop, calls=%fused_computation.2 | loop fusion | flops 50331648 | bytes 50331648 | tf_op jit(solution)/shard_map/concatenate | solution.py:13
  114.4 551.3 %all_to_all.24 = bf16[16,1536,4,128]{3,2,1,0:T(4,128)(2,1)} all-to-all(bf16[16,1536,4,128]{3,2,1,0:T(4,128)(2,1)} %pad_maximum_fusion), channel_id=1, replica_groups=mesh['farcp'=4,'nearcp'=4,'heads'=2] {'farcp','nearcp'}, dimensions={0} | all-to-all | bytes 50331648 | tf_op jit(solution)/shard_map/all_to_all | solution.py:29
  665.7 5.6 all-to-all-start.1
  671.3 38.5 %copy.10 = bf16[1,24576,4,128]{1,3,2,0:T(8,128)(2,1)} copy(bf16[1,24576,4,128]{3,2,1,0:T(4,128)(2,1)} %bitcast.6) | data formatting | bytes 50331648 | tf_op jit(solution)/shard_map/all_to_all | solution.py:29
  709.8 19.2 %fusion = (bf16[384,4,128]{2,1,0:T(4,128)(2,1)}, bf16[384,4,128]{2,1,0:T(4,128)(2,1)}) fusion(bf16[1,384,64,4,128]{4,3,2,1,0:T(4,128)(2,1)} %bitcast.7), kind=kLoop, calls=%fused_computation.5 | loop fusion | flops 24772608 | bytes 25952256 | tf_op jit(solution)/shard_map/reduce_min | solution.py:36
  729.0 486.0 %all-to-all-done.1 = bf16[16,1536,4,128]{3,2,1,0:T(4,128)(2,1)} async-done(((bf16[16,1536,4,128]{3,2,1,0:T(4,128)(2,1)}), bf16[16,1536,4,128]{3,2,1,0:T(4,128)(2,1)}, u32[]{:S(2)}, u32[]{:S(2)}) %all-to-all-start.1) | async-done | bytes 25165856 | tf_op jit(solution)/shard_map/all_to_all | solution.py:30
  1215.0 17.2 %copy.12 = bf16[1,24576,4,128]{3,2,1,0:T(4,128)(2,1)} copy(bf16[1,24576,4,128]{3,2,1,0:T(4,128)(2,1)} %bitcast.2) | data formatting | bytes 50331648
Async XLA Ops:
  665.7 549.3 %all-to-all-start.1 = ((bf16[16,1536,4,128]{3,2,1,0:T(4,128)(2,1)}), bf16[16,1536,4,128]{3,2,1,0:T(4,128)(2,1)}, u32[]{:S(2)}, u32[]{:S(2)}) async-start(bf16[16,1536,4,128]{3,2,1,0:T(4,128)(2,1)} %param.4), calls=%async_computation.1 | async-start | bytes 50331648 | tf_op jit(solution)/shard_map/all_to_all | solution.py:30
where the time goes:
time: 1230 us
  blocking collectives  551 us (45%)
  waiting for transfers between devices  486 us (40%)
  other arithmetic  130 us (11%)
  local copies, waits for them, and re-layouts  58.5 us (5%)
    all_to_all x1, blocking collectives, per_device(): lax.all_to_all(sent_keys, ('farcp', 'nearcp'), split_axis=0, concat_axis=...  551 us
    all_to_all x1, waiting for transfers between devices, per_device(): lax.all_to_all(raw_values, ('farcp', 'nearcp'), split_axis=0, concat_axis...  486 us
    another operation x1, other arithmetic  49.4 us
    all_to_all x1, local copies, waits for them, and re-layouts, per_device(): lax.all_to_all(sent_keys, ('farcp', 'nearcp'), split_axis=0, concat_axis=...  38.5 us
    concatenate x1, other arithmetic, apply_rotary(): jnp.concatenate([first * cosine - second * sine, second * cosine + first...  37.5 us
  transfers between devices with their start and end apart: 1, of which 1 were waited for; matrix products, arithmetic and copies ran while one was open for 5% of the time, Pallas kernels for 0%

commit v1 on v0

v1 whole, which is shorter than its diff:
```python
import functools

import jax
import jax.numpy as jnp
from jax import lax
from jax.experimental import pallas as pl
from jax.experimental.pallas import tpu as pltpu
from jax.sharding import PartitionSpec as P

PAGE = 64
AXES = ("farcp", "nearcp")
BLOCK = 256


def apply_rotary(vectors, angle):
    half = vectors.shape[-1] // 2
    cosine, sine = (jnp.cos(angle)[None, :, None, :], jnp.sin(angle)[None, :, None, :])
    first, second = (vectors[..., :half], vectors[..., half:])
    return jnp.concatenate(
        [first * cosine - second * sine, second * cosine + first * sine], axis=-1
    )


def exchange(array):
    return lax.all_to_all(array, AXES, split_axis=0, concat_axis=0, tiled=True)


def finish_kernel(heads, size, chunk_ref, *refs):
    keys_ref, high_ref, low_ref = refs[-3:]
    rows = chunk_ref.shape[1]
    for head in range(heads):
        part = chunk_ref[0, :, head * size : (head + 1) * size]
        keys_ref[0, head] = part.T
        for page in range(rows // PAGE):
            piece = part[page * PAGE : (page + 1) * PAGE]
            high_ref[0, page, head : head + 1, :] = jnp.max(piece, axis=0, keepdims=True)
            low_ref[0, page, head : head + 1, :] = jnp.min(piece, axis=0, keepdims=True)


def finish(chunk, before, start, span, heads, size):
    sources, rows, lanes = chunk.shape
    length = sources * span
    steps = rows // BLOCK
    where = lambda s, b: s * (span // BLOCK) + start // BLOCK + b
    outs = (
        jax.ShapeDtypeStruct((1, heads, size, length), chunk.dtype),
        jax.ShapeDtypeStruct((1, length // PAGE, heads, size), chunk.dtype),
        jax.ShapeDtypeStruct((1, length // PAGE, heads, size), chunk.dtype),
    )
    page_spec = pl.BlockSpec(
        (1, BLOCK // PAGE, heads, size), lambda s, b: (0, where(s, b), 0, 0)
    )
    in_specs = [pl.BlockSpec((1, BLOCK, lanes), lambda s, b: (s, b, 0))]
    in_specs += [pl.BlockSpec(memory_space=pl.ANY)] * len(before)
    return pl.pallas_call(
        functools.partial(finish_kernel, heads, size),
        grid=(sources, steps),
        in_specs=in_specs,
        out_specs=(
            pl.BlockSpec((1, heads, size, BLOCK), lambda s, b: (0, 0, 0, where(s, b))),
            page_spec,
            page_spec,
        ),
        out_shape=outs,
        input_output_aliases={1 + i: i for i in range(len(before))},
        cost_estimate=pl.CostEstimate(
            flops=4 * chunk.size, bytes_accessed=4 * chunk.size, transcendentals=0
        ),
        name=f"finish_{start}",
    )(chunk, *before)


def place_kernel(from_ref, to_ref):
    to_ref[...] = from_ref[...]


def place(array):
    spec = pl.BlockSpec((1,) + array.shape[1:], lambda s: (s, 0, 0, 0))
    return pl.pallas_call(
        place_kernel,
        grid=(array.shape[0],),
        in_specs=[spec],
        out_specs=spec,
        out_shape=jax.ShapeDtypeStruct(array.shape, array.dtype),
        cost_estimate=pl.CostEstimate(
            flops=0, bytes_accessed=4 * array.size, transcendentals=0
        ),
        name="place",
    )(array)


def per_device(raw_keys, raw_values, turn_angle):
    batch, span, heads, size = raw_keys.shape
    moved_values = exchange(raw_values)
    my_angles = lax.dynamic_slice_in_dim(turn_angle, lax.axis_index(AXES) * span, span)
    turned = apply_rotary(raw_keys.astype(jnp.float32), my_angles).astype(jnp.bfloat16)
    turned = turned.reshape(batch, span, heads * size)
    cut = span - BLOCK
    bounds = [(0, cut), (cut, span)] if cut else [(0, span)]
    pieces = [turned[:, first:last] for first, last in bounds]
    pieces, moved_values = lax.optimization_barrier((pieces, moved_values))
    arrived = exchange(pieces[0])
    stored_values = place(moved_values)
    done = finish(arrived, (), 0, span, heads, size)
    if cut:
        last, _, stored_values = lax.optimization_barrier((pieces[1], arrived, stored_values))
        done = finish(exchange(last), done, cut, span, heads, size)
    stored_values = stored_values.reshape(1, -1, heads, size)
    return (done[0], stored_values, done[1], done[2])


def solution(mesh):
    return jax.shard_map(
        per_device,
        mesh=mesh,
        in_specs=(
            P(None, AXES, "heads", None),
            P(None, AXES, "heads", None),
            P(),
        ),
        out_specs=(
            P(AXES, "heads", None, None),
            P(AXES, None, "heads", None),
            P(AXES, None, "heads", None),
            P(AXES, None, "heads", None),
        ),
        check_vma=False,
    )
```

time: 1230 us -> 1120 us (0.911)
  blocking collectives: 551 us -> 0 us
  waiting for transfers between devices: 486 us -> 848 us
  Pallas kernels: 0 us -> 82.2 us
  other arithmetic: 130 us -> 111 us
    all_to_all x1 -> x0, blocking collectives: 551 us -> none  [per_device(): lax.all_to_all(sent_keys, ('farcp', 'nearcp'), split_axis=0, concat_axis=...]
    all_to_all x1 -> x3, waiting for transfers between devices: 486 us -> 848 us  [exchange(): return lax.all_to_all(array, AXES, split_axis=0, concat_axis=0, tiled=True)]
    pallas_call x0 -> x3, Pallas kernels: none -> 82.2 us  [the longest x2 60 us: finish(): pl.pallas_call(functools.partial(finish_kernel, heads, size), grid=(sourc...]
    all_to_all x1 -> x0, local copies, waits for them, and re-layouts: 38.5 us -> none  [per_device(): lax.all_to_all(sent_keys, ('farcp', 'nearcp'), split_axis=0, concat_axis=...]
    convert_element_type x0 -> x1, local copies, waits for them, and re-layouts: none -> 36.6 us  [per_device(): apply_rotary(raw_keys.astype(jnp.float32), my_angles).astype(jnp.bfloat16)]
    slice x0 -> x2, local copies, waits for them, and re-layouts: none -> 21.7 us  [per_device(): pieces = [turned[:, first:last] for first, last in bounds]]
    reduce_min x1 -> x0, other arithmetic: 19.2 us -> none  [per_device(): page_low = jnp.min(page_view, axis=2)]
    unnamed x1 -> x0, local copies, waits for them, and re-layouts: 17.2 us -> none
  transfers between devices with their start and end apart: 1 -> 3, of which waited for: 1 -> 3; matrix products, arithmetic and copies ran while one was open for 5% -> 15% of each run, Pallas kernels for 0% -> 6%
where the time goes in v1:
time: 1120 us
  waiting for transfers between devices  848 us (76%)
  other arithmetic  111 us (10%)
  Pallas kernels  82.2 us (7%)
  local copies, waits for them, and re-layouts  61.1 us (5%)
  starting transfers between devices  15.9 us (1%)
    all_to_all x3, waiting for transfers between devices, exchange(): return lax.all_to_all(array, AXES, split_axis=0, concat_axis=0, tiled=True)  848 us
    pallas_call x2, Pallas kernels, finish(): pl.pallas_call(functools.partial(finish_kernel, heads, size), grid=(sourc...  60 us
    another operation x1, other arithmetic  49.4 us
    concatenate x1, other arithmetic, apply_rotary(): jnp.concatenate([first * cosine - second * sine, second * cosine + first...  37.6 us
    convert_element_type x1, local copies, waits for them, and re-layouts, per_device(): apply_rotary(raw_keys.astype(jnp.float32), my_angles).astype(jnp.bfloat16)  36.6 us
    convert_element_type x1, other arithmetic, per_device(): raw_keys.astype(jnp.float32)  23.9 us
  transfers between devices with their start and end apart: 3, of which 3 were waited for; matrix products, arithmetic and copies ran while one was open for 15% of the time, Pallas kernels for 6%

profile of v1, /device:TPU:4, one launch (start us, length us, event | category | flops | bytes accessed | tf_op | source)
XLA Modules:
  0.0 1119.2 jit_solution(15183632646121614919)
XLA Ops:
  0.6 6.0 all-to-all-start
  6.6 2.3 dynamic-slice_cosine_fusion
  9.0 0.3 copy.10
  9.2 0.3 copy.11
  9.5 23.9 %convert_element_type.8 = f32[16,1536,4,128]{3,2,1,0:T(4,128)} convert(bf16[16,1536,4,128]{3,2,1,0:T(4,128)(2,1)} %param.3) | non-fusion elementwise | flops 12582912 | bytes 75497472 | tf_op jit(solution)/shard_map/convert_element_type | solution.py:96
  33.4 49.4 %subtract_convert_fusion = (bf16[16,1536,4,64]{3,2,1,0:T(4,128)(2,1)}, bf16[16,1536,4,64]{3,2,1,0:T(4,128)(2,1)}) fusion(f32[16,1536,4,128]{3,2,1,0:T(4,128)} %convert_element_type.8, f32[1536,64]{1,0:T(8,128)S(1)} %copy.11, f32[1536,64]{1,0:T(8,128)S(1)} %copy.10), kind=kLoop, calls=%fused_computation.1 | loop fusion | flops 50331648 | bytes 76283904 | tf_op jit(solution)/shard_map/convert
  82.9 37.6 %pad_maximum_fusion = bf16[16,1536,4,128]{3,2,1,0:T(4,128)(2,1)} fusion(bf16[16,1536,4,64]{3,2,1,0:T(4,128)(2,1)} %get-tuple-element.27, bf16[16,1536,4,64]{3,2,1,0:T(4,128)(2,1)} %get-tuple-element.26), kind=kLoop, calls=%fused_computation.2 | loop fusion | flops 50331648 | bytes 50331648 | tf_op jit(solution)/shard_map/concatenate | solution.py:19
  120.4 36.6 %convert_element_type.9 = bf16[16,1536,512]{2,1,0:T(8,128)(2,1)} reshape(bf16[16,1536,4,128]{3,2,1,0:T(4,128)(2,1)} %pad_maximum_fusion) | data formatting | bytes 50331648 | tf_op jit(solution)/shard_map/convert_element_type | solution.py:96
  157.0 17.2 %slice.18 = bf16[16,1280,512]{2,1,0:T(8,128)(2,1)} slice(bf16[16,1536,512]{2,1,0:T(8,128)(2,1)} %convert_element_type.9), slice={[0:16], [0:1280], [0:512]} | slice | bytes 41943040 | tf_op jit(solution)/shard_map/slice | solution.py:100
  174.2 4.5 slice.19
  178.7 371.6 %all-to-all-done.from_ref = bf16[16,1536,4,128]{3,2,1,0:T(4,128)(2,1)} async-done(((bf16[16,1536,4,128]{3,2,1,0:T(4,128)(2,1)}), bf16[16,1536,4,128]{3,2,1,0:T(4,128)(2,1)}, u32[]{:S(2)}, u32[]{:S(2)}) %all-to-all-start) | async-done | bytes 25165856 | tf_op jit(solution)/shard_map/all_to_all | solution.py:25
  550.3 5.4 all-to-all-start.1
  555.7 22.3 %place.1 = bf16[16,1536,4,128]{3,2,1,0:T(4,128)(2,1)} custom-call(bf16[16,1536,4,128]{3,2,1,0:T(4,128)(2,1)} %all-to-all-done.from_ref), custom_call_target="tpu_custom_call" | custom-call | bytes 50331648 | tf_op jit(solution)/shard_map/place/pallas_call | solution.py:79
  578.0 431.5 %all-to-all-done.1.chunk_ref = bf16[16,1280,512]{2,1,0:T(8,128)(2,1)} async-done(((bf16[16,1280,512]{2,1,0:T(8,128)(2,1)}), bf16[16,1280,512]{2,1,0:T(8,128)(2,1)}, u32[]{:S(2)}, u32[]{:S(2)}) %all-to-all-start.1) | async-done | bytes 20971552 | tf_op jit(solution)/shard_map/all_to_all | solution.py:25
  1009.5 4.6 all-to-all-start.2
  1014.1 49.1 %finish_0.1 = (bf16[1,4,128,24576]{3,2,1,0:T(8,128)(2,1)}, bf16[1,384,4,128]{3,2,1,0:T(4,128)(2,1)}, bf16[1,384,4,128]{3,2,1,0:T(4,128)(2,1)}) custom-call(bf16[16,1280,512]{2,1,0:T(8,128)(2,1)} %all-to-all-done.1.chunk_ref), custom_call_target="tpu_custom_call" | custom-call | flops 41943040 | bytes 41943040 | tf_op jit(solution)/shard_map/finish_0/pallas_call | solution.py:55
  1063.2 45.2 %all-to-all-done.2.chunk_ref = bf16[16,256,512]{2,1,0:T(8,128)(2,1)} async-done(((bf16[16,256,512]{2,1,0:T(8,128)(2,1)}), bf16[16,256,512]{2,1,0:T(8,128)(2,1)}, u32[]{:S(2)}, u32[]{:S(2)}) %all-to-all-start.2) | async-done | bytes 4194336 | tf_op jit(solution)/shard_map/all_to_all | solution.py:25
  1108.4 10.8 finish_1280.1
Async XLA Ops:
  0.6 549.7 %all-to-all-start = ((bf16[16,1536,4,128]{3,2,1,0:T(4,128)(2,1)}), bf16[16,1536,4,128]{3,2,1,0:T(4,128)(2,1)}, u32[]{:S(2)}, u32[]{:S(2)}) async-start(bf16[16,1536,4,128]{3,2,1,0:T(4,128)(2,1)} %param.4), calls=%async_computation | async-start | bytes 50331648 | tf_op jit(solution)/shard_map/all_to_all | solution.py:25
  550.3 459.2 %all-to-all-start.1 = ((bf16[16,1280,512]{2,1,0:T(8,128)(2,1)}), bf16[16,1280,512]{2,1,0:T(8,128)(2,1)}, u32[]{:S(2)}, u32[]{:S(2)}) async-start(bf16[16,1280,512]{2,1,0:T(8,128)(2,1)} %slice.18), calls=%async_computation.1 | async-start | bytes 41943040 | tf_op jit(solution)/shard_map/all_to_all | solution.py:25
  1009.5 98.9 %all-to-all-start.2 = ((bf16[16,256,512]{2,1,0:T(8,128)(2,1)}), bf16[16,256,512]{2,1,0:T(8,128)(2,1)}, u32[]{:S(2)}, u32[]{:S(2)}) async-start(bf16[16,256,512]{2,1,0:T(8,128)(2,1)} %slice.19), calls=%async_computation.2 | async-start | bytes 8388608 | tf_op jit(solution)/shard_map/all_to_all | solution.py:25
